TPU v7x, 32 devices: a whole 2x2x4 slice. The times are simulated.
32 devices in a mesh: dp: 8 (over y, x, core), mp: 4 (over z).
Axes of the slice: x: 2, y: 2, z: 4, core: 2. Of those that a mesh axis runs over, the one named last changes fastest.
Arguments:
- query_new: bfloat16 [32, 4096], P(('dp', 'mp')), parts along dimension 0, may hold values from -140 to 140
- key_new: bfloat16 [32, 1024], P(('dp', 'mp')), parts along dimension 0, may hold values from -5 to 5
- value_new: bfloat16 [32, 1024], P(('dp', 'mp')), parts along dimension 0, may hold values from -5 to 5
- prefix_keys: bfloat16 [4096, 1024], P(('dp', 'mp')), parts along dimension 0, may hold values from -5 to 5
- prefix_values: bfloat16 [4096, 1024], P(('dp', 'mp')), parts along dimension 0, may hold values from -5 to 5
- sample_suffix_keys: bfloat16 [32, 64, 1024], P(('dp', 'mp')), parts along dimension 0, may hold values from -5 to 5
- sample_suffix_values: bfloat16 [32, 64, 1024], P(('dp', 'mp')), parts along dimension 0, may hold values from -5 to 5
- prefix_len: int32 [8], P('dp'), parts along dimension 0, may hold values from 128 to 512
- suffix_len: int32 [32], P(('dp', 'mp')), parts along dimension 0, may hold values from 1 to 64, as said below
- residual: bfloat16 [32, 8192], P(('dp', 'mp')), parts along dimension 0, may hold values from -3 to 3
- out_weight: bfloat16 [4096, 8192], P('mp'), may hold values from -0.1875 to 0.1875
- norm_gain: bfloat16 [8192], replicated, may hold values from 0.5 to 1.5
Outputs:
- hidden: bfloat16 [32, 8192], P(('dp', 'mp')), parts along dimension 0
- normed: bfloat16 [32, 8192], P(('dp', 'mp')), parts along dimension 0
There are 8 independent parts, one for each index of `dp`. A program takes and returns all parts, laid end to end along the dimension named above; an argument that names none is the same for every part. Nothing has to cross between parts.
Inputs may be any that keep to these rules, and one draw needn't show every extreme that they name: `suffix_len`: some sample has exactly 64 cached generated tokens.
All inputs are finite; a program needn't handle non-finite values.
Results may differ from a plain program's by a relative error of at most 0.0085.
Values may be sent and summed in bfloat16 or wider, within the bound.
A program may use at most 64 MiB of HBM per device.

v0:
```python
import jax
import jax.numpy as jnp
from jax import lax
from jax.sharding import PartitionSpec as P

HEAD_SIZE = 128
KEY_VALUE_HEADS = 8
HQ = 32


def local(
    query_new,
    key_new,
    value_new,
    prefix_keys,
    prefix_values,
    sample_suffix_keys,
    sample_suffix_values,
    prefix_len,
    suffix_len,
    residual,
    out_weight,
    norm_gain,
):
    count_mp = lax.axis_size("mp")
    place = lax.axis_index("mp")
    samples_per_part = query_new.shape[0]
    batch = samples_per_part * count_mp
    heads_dev = out_weight.shape[0] // HEAD_SIZE
    group = HQ // KEY_VALUE_HEADS
    pre_dev = prefix_keys.shape[0]
    suffix_result = sample_suffix_keys.shape[1]
    score_scale = HEAD_SIZE ** (-0.5)
    first_row = place * samples_per_part
    queries = lax.all_gather(query_new, "mp", axis=0, tiled=True)
    query_all = queries.reshape(batch, KEY_VALUE_HEADS, group, HEAD_SIZE)
    pkeys = prefix_keys.reshape(pre_dev, KEY_VALUE_HEADS, HEAD_SIZE)
    prefix_value_rows = prefix_values.reshape(pre_dev, KEY_VALUE_HEADS, HEAD_SIZE)
    s_pre = (
        jnp.einsum("bkgd,pkd->bkgp", query_all, pkeys, preferred_element_type=jnp.float32)
        * score_scale
    )
    positions = place * pre_dev + lax.iota(jnp.int32, pre_dev)
    pvalid = (positions < prefix_len[0])[None, None, None, :]
    s_pre = jnp.where(pvalid, s_pre, -jnp.inf)
    query_sample_rows = query_new.reshape(samples_per_part, KEY_VALUE_HEADS, group, HEAD_SIZE)
    suffix_key_rows = sample_suffix_keys.reshape(
        samples_per_part, suffix_result, KEY_VALUE_HEADS, HEAD_SIZE
    )
    suffix_value_rows = sample_suffix_values.reshape(
        samples_per_part, suffix_result, KEY_VALUE_HEADS, HEAD_SIZE
    )
    nvals = value_new.reshape(samples_per_part, KEY_VALUE_HEADS, HEAD_SIZE)
    suffix_score_rows = (
        jnp.einsum(
            "cqxt,caqt->cqxa",
            query_sample_rows,
            suffix_key_rows,
            preferred_element_type=jnp.float32,
        )
        * score_scale
    )
    svalid = (lax.iota(jnp.int32, suffix_result)[None, :] < suffix_len[:, None])[:, None, None, :]
    suffix_score_rows = jnp.where(svalid, suffix_score_rows, -jnp.inf)
    fresh_score_rows = (
        jnp.einsum(
            "exio,exo->exi",
            query_sample_rows,
            key_new.reshape(samples_per_part, KEY_VALUE_HEADS, HEAD_SIZE),
            preferred_element_type=jnp.float32,
        )
        * score_scale
    )
    top_pre = jnp.maximum(jnp.max(s_pre, -1), -1e30)
    own_top = lax.dynamic_slice_in_dim(top_pre, first_row, samples_per_part, 0)
    own_top = jnp.maximum(jnp.maximum(own_top, jnp.max(suffix_score_rows, -1)), fresh_score_rows)
    local_top = lax.dynamic_update_slice_in_dim(top_pre, own_top, first_row, 0)
    top_own = lax.dynamic_slice_in_dim(local_top, first_row, samples_per_part, 0)
    w_pre = jnp.where(pvalid, jnp.exp(s_pre - local_top[..., None]), 0.0)
    total = jnp.sum(w_pre, -1)
    summed_rows = jnp.einsum(
        "wnso,onr->wnsr",
        w_pre.astype(jnp.bfloat16),
        prefix_value_rows,
        preferred_element_type=jnp.float32,
    )
    suffix_weight_rows = jnp.where(svalid, jnp.exp(suffix_score_rows - top_own[..., None]), 0.0)
    w_new = jnp.exp(fresh_score_rows - top_own)
    own_total = jnp.sum(suffix_weight_rows, -1) + w_new
    own_sum = jnp.einsum(
        "cjax,cxjq->cjaq",
        suffix_weight_rows.astype(jnp.bfloat16),
        suffix_value_rows,
        preferred_element_type=jnp.float32,
    )
    own_sum = (
        own_sum
        + w_new.astype(jnp.bfloat16).astype(jnp.float32)[..., None]
        * nvals.astype(jnp.float32)[:, :, None, :]
    )
    total = lax.dynamic_update_slice_in_dim(
        total,
        lax.dynamic_slice_in_dim(total, first_row, samples_per_part, 0) + own_total,
        first_row,
        0,
    )
    summed_rows = lax.dynamic_update_slice_in_dim(
        summed_rows,
        lax.dynamic_slice_in_dim(summed_rows, first_row, samples_per_part, 0) + own_sum,
        first_row,
        0,
    )
    top_flat = local_top.reshape(batch, HQ)
    total_flat = total.reshape(batch, HQ)
    summed_flat = summed_rows.reshape(batch, HQ, HEAD_SIZE)
    parts = (
        lax.all_to_all(top_flat[None], "mp", split_axis=2, concat_axis=0, tiled=True),
        lax.all_to_all(total_flat[None], "mp", split_axis=2, concat_axis=0, tiled=True),
        lax.all_to_all(summed_flat[None], "mp", split_axis=2, concat_axis=0, tiled=True),
    )
    best = jnp.max(parts[0], axis=0)
    factor = jnp.exp(parts[0] - best[None])
    whole_total = jnp.sum(factor * parts[1], axis=0)
    whole_summed = jnp.sum(factor[..., None] * parts[2], axis=0)
    items = parts[0].shape[1]
    attn = (
        (whole_summed / whole_total[..., None])
        .astype(jnp.bfloat16)
        .reshape(items, heads_dev * HEAD_SIZE)
    )
    proj = lax.psum_scatter(
        jnp.dot(attn, out_weight, preferred_element_type=jnp.float32),
        "mp",
        scatter_dimension=0,
        tiled=True,
    )
    stream = residual.astype(jnp.float32) + proj
    hidden = stream.astype(jnp.bfloat16)
    meansq = jnp.mean(stream * stream, axis=-1, keepdims=True)
    normed = (stream * lax.rsqrt(meansq + 1e-05) * norm_gain.astype(jnp.float32)[None, :]).astype(
        jnp.bfloat16
    )
    return (hidden, normed)


def solution(mesh):
    placed = (
        P(("dp", "mp"), None),
        P(("dp", "mp"), None),
        P(("dp", "mp"), None),
        P(("dp", "mp"), None),
        P(("dp", "mp"), None),
        P(("dp", "mp"), None, None),
        P(("dp", "mp"), None, None),
        P("dp"),
        P(("dp", "mp")),
        P(("dp", "mp"), None),
        P("mp", None),
        P(),
    )
    return jax.shard_map(
        local,
        mesh=mesh,
        in_specs=placed,
        out_specs=(P(("dp", "mp"), None), P(("dp", "mp"), None)),
        check_vma=False,
    )
```

profile of v0, /device:TPU:0, one launch (start us, length us, event | category | flops | bytes accessed | tf_op | source)
XLA Modules:
  0.0 110.2 jit_solution(15643182920238004057)
XLA Ops:
  7.9 1.0 copy.106
  8.9 15.1 %all-gather = bf16[4,1,4096]{2,1,0:T(2,128)(2,1)S(1)} all-gather(bf16[1,1,4096]{2,1,0:T(2,128)(2,1)} %bitcast.113), channel_id=1, replica_groups=mesh['dp'=8,'mp'=4] {'mp'}, dimensions={0}, use_global_device_ids=true | all-gather | bytes 40960 | tf_op jit(solution)/shard_map/all_gather | solution.py:35
  24.0 0.8 reduce.7
  24.8 0.2 reduce.6
  25.0 0.3 fusion.39
  25.4 0.1 copy.68
  26.2 0.9 copy.107
  27.1 0.2 fusion.40
  27.4 0.1 fusion.31
  27.7 0.1 copy.76
  27.8 0.2 fusion.12
  28.2 0.2 fusion.19
  28.6 0.7 copy.101
  29.3 4.7 %all-to-all-start.2 = ((f32[1,4,32]{1,0,2:T(1,128)}), f32[1,4,32]{1,0,2:T(1,128)S(1)}, u32[]{:S(2)}, u32[]{:S(2)}) async-start(f32[1,4,32]{1,0,2:T(1,128)} %bitcast.25), calls=%async_computation.2 | async-start | bytes 32768 | tf_op jit(solution)/shard_map/all_to_all | solution.py:118
  34.0 1.0 copy.108
  35.0 0.3 fusion.6
  35.3 0.7 copy.97
  36.1 0.9 copy.109
  37.0 0.7 convert_element_type.50
  37.7 1.9 %all-to-all-done.2 = f32[1,4,32]{1,0,2:T(1,128)S(1)} async-done(((f32[1,4,32]{1,0,2:T(1,128)}), f32[1,4,32]{1,0,2:T(1,128)S(1)}, u32[]{:S(2)}, u32[]{:S(2)}) %all-to-all-start.2) | async-done | bytes 544 | tf_op jit(solution)/shard_map/all_to_all | solution.py:118
  39.7 3.3 %all-to-all-start = ((f32[1,4,32]{1,0,2:T(1,128)}), f32[1,4,32]{1,0,2:T(1,128)S(1)}, u32[]{:S(2)}, u32[]{:S(2)}) async-start(f32[1,4,32]{1,0,2:T(1,128)} %bitcast.9), calls=%async_computation | async-start | bytes 32768 | tf_op jit(solution)/shard_map/all_to_all | solution.py:117
  42.9 0.2 fusion.4
  43.2 0.7 copy.82
  43.9 4.6 %all-to-all-done = f32[1,4,32]{1,0,2:T(1,128)S(1)} async-done(((f32[1,4,32]{1,0,2:T(1,128)}), f32[1,4,32]{1,0,2:T(1,128)S(1)}, u32[]{:S(2)}, u32[]{:S(2)}) %all-to-all-start) | async-done | bytes 544 | tf_op jit(solution)/shard_map/all_to_all | solution.py:117
  48.5 3.3 %all-to-all-start.1 = ((f32[1,4,32,128]{3,1,0,2:T(4,128)}), f32[1,4,32,128]{3,1,0,2:T(4,128)S(1)}, u32[]{:S(2)}, u32[]{:S(2)}) async-start(f32[1,4,32,128]{3,1,0,2:T(4,128)} %copy.82), calls=%async_computation.1 | async-start | bytes 131072 | tf_op jit(solution)/shard_map/all_to_all | solution.py:119
  51.8 0.1 copy.98
  52.0 5.5 %all-to-all-done.1 = f32[1,4,32,128]{3,1,0,2:T(4,128)S(1)} async-done(((f32[1,4,32,128]{3,1,0,2:T(4,128)}), f32[1,4,32,128]{3,1,0,2:T(4,128)S(1)}, u32[]{:S(2)}, u32[]{:S(2)}) %all-to-all-start.1) | async-done | bytes 65568 | tf_op jit(solution)/shard_map/all_to_all | solution.py:119
  57.7 8.7 %fusion.22 = f32[4,8192]{1,0:T(4,128)} fusion(bf16[1024,8192]{1,0:T(8,128)(2,1)} %param.22, bf16[1,4,8,128]{3,2,1,0:T(8,128)(2,1)S(1)} %fusion.29), kind=kOutput, calls=%fused_computation.30 | convolution fusion | flops 67108864 | bytes 16916480 | tf_op jit(solution)/shard_map/dot_general | solution.py:132
  66.4 0.6 dynamic-slice.4
  67.0 32.7 %all-reduce.3.cloned.1.call-done = f32[4,8192]{1,0:T(4,128)} async-done(((f32[4,8192]{1,0:T(4,128)}), f32[4,8192]{1,0:T(4,128)}) %all-reduce.3.cloned.1.call-update) | async-done | bytes 131088
  99.8 2.2 %multiply_reduce_fusion = (f32[]{:T(128)}, f32[1,8192]{1,0:T(1,128)S(1)}) fusion(f32[4,8192]{1,0:T(4,128)} %all-reduce.3.cloned.1.call-done, u32[]{:T(128)} %bitcast.33, bf16[1,8192]{1,0:T(2,128)(2,1)S(1)} %copy-done.1), kind=kLoop, calls=%fused_computation.22 | loop fusion | flops 32767 | bytes 81928 | tf_op jit(solution)/shard_map/reduce_sum | solution.py:139
  102.7 0.7 multiply_convert_fusion
  (35 shorter events, 1.1 us)
Async XLA Ops:
  7.2 20.2 %copy-start = (bf16[1,1024]{1,0:T(2,128)(2,1)S(1)}, bf16[1,1024]{1,0:T(2,128)(2,1)}, u32[]{:S(2)}) copy-start(bf16[1,1024]{1,0:T(2,128)(2,1)} %param.13) | copy-start | bytes 6148
  7.2 59.2 %copy-start.3 = (u32[32]{0:T(128)S(1)}, u32[32]{0:T(128)}, u32[]{:S(2)}) copy-start(u32[32]{0:T(128)} %constant.37) | copy-start | bytes 388
  7.2 59.2 %copy-start.2 = (bf16[8192]{0:T(1024)(128)(2,1)S(1)}, bf16[8192]{0:T(1024)(128)(2,1)}, u32[]{:S(2)}) copy-start(bf16[8192]{0:T(1024)(128)(2,1)} %param.23) | copy-start | bytes 49156
  7.2 92.6 %copy-start.1 = (bf16[1,8192]{1,0:T(2,128)(2,1)S(1)}, bf16[1,8192]{1,0:T(2,128)(2,1)}, u32[]{:S(2)}) copy-start(bf16[1,8192]{1,0:T(2,128)(2,1)} %param.21) | copy-start | bytes 49156
  29.3 10.3 %all-to-all-start.2 = ((f32[1,4,32]{1,0,2:T(1,128)}), f32[1,4,32]{1,0,2:T(1,128)S(1)}, u32[]{:S(2)}, u32[]{:S(2)}) async-start(f32[1,4,32]{1,0,2:T(1,128)} %bitcast.25), calls=%async_computation.2 | async-start | bytes 32768 | tf_op jit(solution)/shard_map/all_to_all | solution.py:118
  39.7 8.8 %all-to-all-start = ((f32[1,4,32]{1,0,2:T(1,128)}), f32[1,4,32]{1,0,2:T(1,128)S(1)}, u32[]{:S(2)}, u32[]{:S(2)}) async-start(f32[1,4,32]{1,0,2:T(1,128)} %bitcast.9), calls=%async_computation | async-start | bytes 32768 | tf_op jit(solution)/shard_map/all_to_all | solution.py:117
  48.5 9.0 %all-to-all-start.1 = ((f32[1,4,32,128]{3,1,0,2:T(4,128)}), f32[1,4,32,128]{3,1,0,2:T(4,128)S(1)}, u32[]{:S(2)}, u32[]{:S(2)}) async-start(f32[1,4,32,128]{3,1,0,2:T(4,128)} %copy.82), calls=%async_computation.1 | async-start | bytes 131072 | tf_op jit(solution)/shard_map/all_to_all | solution.py:119
  51.8 48.0 %all-reduce.3.cloned.1.call-start = ((), (), s32[]{:S(2)}) async-start(), calls=%async_computation.3 | async-start | bytes 262144
Sparse Core Ops, SparseCore 0:
  66.5 33.1 all-reduce.2
where the time goes:
time: 111 us; the launch traced here: 110 us
  waiting for transfers between devices  44.8 us (40%)
  between operations  16.2 us (15%)
  blocking collectives  15.1 us (14%)
  starting transfers between devices  11.3 us (10%)
  matrix products  9.91 us (9%)
  local copies, waits for them, and re-layouts  7.66 us (7%)
  other arithmetic  5.2 us (5%)
    unnamed x2, waiting for transfers between devices  32.7 us
    all_gather x1, blocking collectives, local(): queries = lax.all_gather(query_new, 'mp', axis=0, tiled=True)  15.1 us
    dot_general x1, matrix products, local(): jnp.dot(attn, out_weight, preferred_element_type=jnp.float32)  8.71 us
    all_to_all x1, waiting for transfers between devices, local(): lax.all_to_all(summed_flat[None], 'mp', split_axis=2, concat_axis=0, tile...  5.51 us
    all_to_all x1, starting transfers between devices, local(): lax.all_to_all(total_flat[None], 'mp', split_axis=2, concat_axis=0, tiled...  4.74 us
    all_to_all x1, waiting for transfers between devices, local(): lax.all_to_all(top_flat[None], 'mp', split_axis=2, concat_axis=0, tiled=T...  4.56 us
    unnamed x15, local copies, waits for them, and re-layouts  4.53 us
    all_to_all x1, starting transfers between devices, local(): lax.all_to_all(summed_flat[None], 'mp', split_axis=2, concat_axis=0, tile...  3.28 us
  transfers between devices with their start and end apart: 4, of which 4 were waited for; matrix products, arithmetic and copies ran while one was open for 5% of the time, Pallas kernels for 0%

commit v1 on v0

v1 whole, which is shorter than its diff:
```python
import functools

import jax
import jax.numpy as jnp
from jax import lax
from jax.experimental import pallas as pl
from jax.experimental.pallas import tpu as pltpu
from jax.sharding import PartitionSpec as P

HEAD_SIZE = 128
KEY_VALUE_HEADS = 8
HQ = 32
GROUP = HQ // KEY_VALUE_HEADS
LANES = 128
LOW = -(2.0**100)
CHUNKS = 4
NT = (((1,), (1,)), ((), ()))


def head(ref, k):
    return ref[:, k * HEAD_SIZE : (k + 1) * HEAD_SIZE]


def kernel(
    n,
    plen_ref,
    slen_ref,
    q_hbm,
    kn_hbm,
    vn_hbm,
    pk_hbm,
    pv_hbm,
    sk_hbm,
    sv_hbm,
    res_hbm,
    w_hbm,
    gain_hbm,
    hid_ref,
    nrm_ref,
    qbuf,
    kn,
    vn,
    pk,
    pv,
    sk,
    sv,
    res,
    w,
    gain,
    q_rows,
    m0,
    l0,
    o0,
    pbuf,
    rbuf,
    yacc,
    ysend,
    ybuf,
    local_sem,
    w_sem,
    q_send,
    q_recv,
    p_send,
    p_recv,
    y_send,
    y_recv,
):
    me = lax.axis_index("mp")
    pre = pk.shape[0]
    suf = sk.shape[0]
    rows = pbuf.shape[0]
    part_rows = rows // n
    heads_dev = HQ // n
    width = w.shape[1]
    cw = width // CHUNKS
    crows = cw // LANES
    frows = width // LANES
    scale = HEAD_SIZE ** (-0.5)

    def peer(d):
        return lax.rem(me + d, n)

    local = [
        pltpu.make_async_copy(src, dst, local_sem.at[i])
        for i, (src, dst) in enumerate(
            (
                (q_hbm, qbuf.at[me]),
                (sk_hbm.at[0], sk),
                (kn_hbm, kn),
                (sv_hbm.at[0], sv),
                (vn_hbm, vn),
                (pk_hbm, pk),
                (pv_hbm, pv),
                (res_hbm, res),
                (gain_hbm, gain),
            )
        )
    ]
    for copy in local:
        copy.start()
    w_copies = [
        pltpu.make_async_copy(
            w_hbm.at[:, pl.ds(c * cw, cw)], w.at[:, pl.ds(c * cw, cw)], w_sem.at[c]
        )
        for c in range(CHUNKS)
    ]
    for copy in w_copies:
        copy.start()

    barrier = pltpu.get_barrier_semaphore()
    for d in range(1, n):
        pl.semaphore_signal(
            barrier, inc=1, device_id={"mp": peer(d)}, device_id_type=pl.DeviceIdType.MESH
        )
    pl.semaphore_wait(barrier, n - 1)

    local[0].wait()
    q_copies = []
    for d in range(1, n):
        copy = pltpu.make_async_remote_copy(
            src_ref=qbuf.at[me],
            dst_ref=qbuf.at[me],
            send_sem=q_send.at[d - 1],
            recv_sem=q_recv.at[d - 1],
            device_id={"mp": peer(d)},
            device_id_type=pl.DeviceIdType.MESH,
        )
        copy.start()
        q_copies.append(copy)

    m0[...] = jnp.full(m0.shape, LOW, jnp.float32)
    l0[...] = jnp.zeros(l0.shape, jnp.float32)
    o0[...] = jnp.zeros(o0.shape, jnp.float32)
    own = qbuf[me].astype(jnp.float32).reshape(HQ, HEAD_SIZE)
    own_bf = own.astype(jnp.bfloat16)
    head_of_row = lax.broadcasted_iota(jnp.int32, (HQ, 1), 0) // GROUP
    local[1].wait()
    local[2].wait()
    s_suf = jnp.zeros((HQ, suf), jnp.float32)
    key_rows = jnp.zeros((HQ, HEAD_SIZE), jnp.float32)
    for k in range(KEY_VALUE_HEADS):
        scores = lax.dot_general(own_bf, head(sk, k), NT, preferred_element_type=jnp.float32)
        s_suf = jnp.where(head_of_row == k, scores, s_suf)
        key_rows = jnp.where(head_of_row == k, head(kn, k).astype(jnp.float32), key_rows)
    s_new = jnp.sum(own * key_rows, axis=1, keepdims=True) * scale
    svalid = lax.broadcasted_iota(jnp.int32, (HQ, suf), 1) < slen_ref[0]
    s_suf = jnp.where(svalid, s_suf * scale, LOW)
    top = jnp.maximum(jnp.max(s_suf, axis=1, keepdims=True), s_new)
    w_suf = jnp.where(svalid, jnp.exp(s_suf - top), 0.0)
    w_new = jnp.exp(s_new - top)
    own_total = jnp.sum(w_suf, axis=1, keepdims=True) + w_new
    w_bf = w_suf.astype(jnp.bfloat16)
    local[3].wait()
    local[4].wait()
    own_sum = jnp.zeros((HQ, HEAD_SIZE), jnp.float32)
    value_rows = jnp.zeros((HQ, HEAD_SIZE), jnp.float32)
    for k in range(KEY_VALUE_HEADS):
        sums = jnp.dot(w_bf, head(sv, k), preferred_element_type=jnp.float32)
        own_sum = jnp.where(head_of_row == k, sums, own_sum)
        value_rows = jnp.where(head_of_row == k, head(vn, k).astype(jnp.float32), value_rows)
    own_sum = own_sum + w_new.astype(jnp.bfloat16).astype(jnp.float32) * value_rows
    own_at = pl.ds(me, HQ, stride=n)
    m0[own_at, :] = jnp.broadcast_to(top, (HQ, LANES))
    l0[own_at, :] = jnp.broadcast_to(own_total, (HQ, LANES))
    o0[own_at, :] = own_sum

    local[5].wait()
    local[6].wait()
    for copy in q_copies:
        copy.wait_recv()
    for s in range(n):
        q_rows[pl.ds(s, HQ, stride=n), :] = qbuf[s].astype(jnp.float32).reshape(HQ, HEAD_SIZE)
    q_bf = q_rows[...].astype(jnp.bfloat16)
    per_kv = rows // KEY_VALUE_HEADS
    s_pre = jnp.concatenate(
        [
            lax.dot_general(
                q_bf[k * per_kv : (k + 1) * per_kv],
                head(pk, k),
                NT,
                preferred_element_type=jnp.float32,
            )
            for k in range(KEY_VALUE_HEADS)
        ],
        axis=0,
    )
    pvalid = me * pre + lax.broadcasted_iota(jnp.int32, (rows, pre), 1) < plen_ref[0]
    s_pre = jnp.where(pvalid, s_pre * scale, LOW)
    top0 = m0[...]
    top = jnp.maximum(jnp.max(s_pre, axis=1, keepdims=True), top0)
    top = top.astype(jnp.bfloat16).astype(jnp.float32)
    w_pre = jnp.where(pvalid, jnp.exp(s_pre - top[:, :1]), 0.0)
    keep = jnp.exp(top0 - top)
    total = jnp.sum(w_pre, axis=1, keepdims=True) + l0[...] * keep
    w_bf = w_pre.astype(jnp.bfloat16)
    sums = jnp.concatenate(
        [
            jnp.dot(
                w_bf[k * per_kv : (k + 1) * per_kv],
                head(pv, k),
                preferred_element_type=jnp.float32,
            )
            for k in range(KEY_VALUE_HEADS)
        ],
        axis=0,
    )
    sums = sums + o0[...] * keep
    high = total.astype(jnp.bfloat16).astype(jnp.float32)
    lane = lax.broadcasted_iota(jnp.int32, (rows, LANES), 1)
    stats = jnp.where(lane < 32, top, jnp.where(lane < 64, high, total - high))
    pbuf[:, :LANES] = sums.astype(jnp.bfloat16)
    pbuf[:, LANES:] = stats.astype(jnp.bfloat16)

    p_copies = []
    for d in range(1, n):
        copy = pltpu.make_async_remote_copy(
            src_ref=pbuf.at[pl.ds(pl.multiple_of(peer(d) * part_rows, part_rows), part_rows)],
            dst_ref=rbuf.at[me],
            send_sem=p_send.at[d - 1],
            recv_sem=p_recv.at[d - 1],
            device_id={"mp": peer(d)},
            device_id_type=pl.DeviceIdType.MESH,
        )
        copy.start()
        p_copies.append(copy)
    rbuf[me] = pbuf[pl.ds(pl.multiple_of(me * part_rows, part_rows), part_rows), :]
    for copy in p_copies:
        copy.wait_recv()

    stats = [rbuf[s, :, LANES:].astype(jnp.float32) for s in range(n)]
    tops = [st[:, 0:1] for st in stats]
    best = functools.reduce(jnp.maximum, tops)
    whole_total = jnp.zeros((part_rows, 1), jnp.float32)
    whole_sum = jnp.zeros((part_rows, HEAD_SIZE), jnp.float32)
    for s in range(n):
        factor = jnp.exp(tops[s] - best)
        whole_total = whole_total + factor * (stats[s][:, 32:33] + stats[s][:, 64:65])
        whole_sum = whole_sum + factor * rbuf[s, :, :LANES].astype(jnp.float32)
    attn = whole_sum / whole_total
    attn = jnp.concatenate([attn[h * n : (h + 1) * n] for h in range(heads_dev)], axis=1)
    attn = attn.astype(jnp.bfloat16)

    y_copies = []
    for c in range(CHUNKS):
        w_copies[c].wait()
        y = jnp.dot(attn, w[:, c * cw : (c + 1) * cw], preferred_element_type=jnp.float32)
        for j in range(crows):
            yacc[pl.ds(c * crows + j, n, stride=frows), :] = y[:, j * LANES : (j + 1) * LANES]
        at = pl.ds(c * crows, crows)
        for s in range(n):
            ysend[s, at, :] = yacc[pl.ds(s * frows + c * crows, crows), :].astype(jnp.bfloat16)
        for d in range(1, n):
            copy = pltpu.make_async_remote_copy(
                src_ref=ysend.at[peer(d), at],
                dst_ref=ybuf.at[me, at],
                send_sem=y_send.at[c * (n - 1) + d - 1],
                recv_sem=y_recv.at[c * (n - 1) + d - 1],
                device_id={"mp": peer(d)},
                device_id_type=pl.DeviceIdType.MESH,
            )
            copy.start()
            y_copies.append(copy)

    local[7].wait()
    local[8].wait()
    stream = res[...].astype(jnp.float32).reshape(frows, LANES)
    stream = stream + yacc[pl.ds(pl.multiple_of(me * frows, frows), frows), :]
    for copy in y_copies:
        copy.wait_recv()
    for d in range(1, n):
        stream = stream + ybuf[peer(d)].astype(jnp.float32)
    hid_ref[...] = stream.astype(jnp.bfloat16).reshape(hid_ref.shape)
    meansq = jnp.sum(stream * stream, keepdims=True) / width
    normed = stream * lax.rsqrt(meansq + 1e-05) * gain[...].astype(jnp.float32)
    nrm_ref[...] = normed.astype(jnp.bfloat16).reshape(nrm_ref.shape)
    for copy in q_copies + p_copies + y_copies:
        copy.wait_send()


def local(
    query_new,
    key_new,
    value_new,
    prefix_keys,
    prefix_values,
    sample_suffix_keys,
    sample_suffix_values,
    prefix_len,
    suffix_len,
    residual,
    out_weight,
    norm_gain,
):
    n = lax.axis_size("mp")
    assert query_new.shape[0] == 1
    width = residual.shape[1]
    frows = width // LANES
    rows = HQ * n
    bf, f32 = jnp.bfloat16, jnp.float32
    gain = norm_gain.reshape(frows, LANES)
    smem = pl.BlockSpec(memory_space=pltpu.SMEM)
    hbm = pl.BlockSpec(memory_space=pltpu.HBM)
    vmem = pl.BlockSpec(memory_space=pltpu.VMEM)
    dma = pltpu.SemaphoreType.DMA
    return pl.pallas_call(
        functools.partial(kernel, n),
        out_shape=(
            jax.ShapeDtypeStruct(residual.shape, bf),
            jax.ShapeDtypeStruct(residual.shape, bf),
        ),
        in_specs=[smem, smem] + [hbm] * 10,
        out_specs=(vmem, vmem),
        scratch_shapes=[
            pltpu.VMEM((n,) + query_new.shape, bf),
            pltpu.VMEM(key_new.shape, bf),
            pltpu.VMEM(value_new.shape, bf),
            pltpu.VMEM(prefix_keys.shape, bf),
            pltpu.VMEM(prefix_values.shape, bf),
            pltpu.VMEM(sample_suffix_keys.shape[1:], bf),
            pltpu.VMEM(sample_suffix_values.shape[1:], bf),
            pltpu.VMEM(residual.shape, bf),
            pltpu.VMEM(out_weight.shape, bf),
            pltpu.VMEM(gain.shape, bf),
            pltpu.VMEM((rows, HEAD_SIZE), f32),
            pltpu.VMEM((rows, LANES), f32),
            pltpu.VMEM((rows, LANES), f32),
            pltpu.VMEM((rows, HEAD_SIZE), f32),
            pltpu.VMEM((rows, HEAD_SIZE + LANES), bf),
            pltpu.VMEM((n, rows // n, HEAD_SIZE + LANES), bf),
            pltpu.VMEM((n * frows, LANES), f32),
            pltpu.VMEM((n, frows, LANES), bf),
            pltpu.VMEM((n, frows, LANES), bf),
            dma((9,)),
            dma((CHUNKS,)),
            dma((n - 1,)),
            dma((n - 1,)),
            dma((n - 1,)),
            dma((n - 1,)),
            dma((CHUNKS * (n - 1),)),
            dma((CHUNKS * (n - 1),)),
        ],
        compiler_params=pltpu.CompilerParams(
            collective_id=0, has_side_effects=True, vmem_limit_bytes=40 * 1024 * 1024
        ),
    )(
        prefix_len,
        suffix_len,
        query_new,
        key_new,
        value_new,
        prefix_keys,
        prefix_values,
        sample_suffix_keys,
        sample_suffix_values,
        residual,
        out_weight,
        gain,
    )


def solution(mesh):
    placed = (
        P(("dp", "mp"), None),
        P(("dp", "mp"), None),
        P(("dp", "mp"), None),
        P(("dp", "mp"), None),
        P(("dp", "mp"), None),
        P(("dp", "mp"), None, None),
        P(("dp", "mp"), None, None),
        P("dp"),
        P(("dp", "mp")),
        P(("dp", "mp"), None),
        P("mp", None),
        P(),
    )
    return jax.shard_map(
        local,
        mesh=mesh,
        in_specs=placed,
        out_specs=(P(("dp", "mp"), None), P(("dp", "mp"), None)),
        check_vma=False,
    )
```

time: 111 us -> 30.6 us (0.28)
  waiting for transfers between devices: 44.8 us -> 0 us
  Pallas kernels: 0 us -> 19.7 us
  blocking collectives: 15.1 us -> 0 us
  between operations: 16.2 us -> 1.95 us
  starting transfers between devices: 11.3 us -> 0 us
  matrix products: 9.91 us -> 0 us
  other arithmetic: 5.2 us -> 0 us
    unnamed x2 -> x0, waiting for transfers between devices: 32.7 us -> none
    pallas_call x0 -> x1, Pallas kernels: none -> 19.7 us  [local(): pl.pallas_call(functools.partial(kernel, n), out_shape=(jax.ShapeDtypeStr...]
    all_gather x1 -> x0, blocking collectives: 15.1 us -> none  [local(): queries = lax.all_gather(query_new, 'mp', axis=0, tiled=True)]
    all_to_all x3 -> x0, waiting for transfers between devices: 12 us -> none  [the longest x1 5.51 us: local(): lax.all_to_all(summed_flat[None], 'mp', split_axis=2, concat_axis=0, tile...]
    all_to_all x3 -> x0, starting transfers between devices: 11.3 us -> none  [the longest x1 4.74 us: local(): lax.all_to_all(total_flat[None], 'mp', split_axis=2, concat_axis=0, tiled...]
    dot_general x6 -> x0, matrix products: 9.91 us -> none  [the longest x1 8.71 us: local(): jnp.dot(attn, out_weight, preferred_element_type=jnp.float32)]
    unnamed x15 -> x20, local copies, waits for them, and re-layouts: 4.53 us -> 8.5 us
    reduce_sum x5 -> x0, other arithmetic: 2.72 us -> none  [the longest x1 2.23 us: local(): meansq = jnp.mean(stream * stream, axis=-1, keepdims=True)]
  transfers between devices with their start and end apart: 4 -> 0, of which waited for: 4 -> 0; matrix products, arithmetic and copies ran while one was open for 5% -> 0% of each run, Pallas kernels for 0% -> 0%
where the time goes in v1:
time: 30.6 us; the launch traced here: 30.1 us
  Pallas kernels  19.7 us (64%)
  local copies, waits for them, and re-layouts  8.5 us (28%)
  between operations  1.95 us (6%)
    pallas_call x1, Pallas kernels, local(): pl.pallas_call(functools.partial(kernel, n), out_shape=(jax.ShapeDtypeStr...  19.7 us
    unnamed x20, local copies, waits for them, and re-layouts  8.5 us

profile of v1, /device:TPU:0, one launch (start us, length us, event | category | flops | bytes accessed | tf_op | source)
XLA Modules:
  0.0 30.1 jit_solution(4803664034212563734)
XLA Ops:
  1.9 0.0 copy-start
  1.9 0.9 %copy-done = bf16[128,1024]{1,0:T(8,128)(2,1)S(1)} copy-done((bf16[128,1024]{1,0:T(8,128)(2,1)S(1)}, bf16[128,1024]{1,0:T(8,128)(2,1)}, u32[]{:S(2)}) %copy-start) | copy-done | bytes 262168
  2.9 0.0 copy-start.1
  2.9 0.9 %copy-done.1 = bf16[128,1024]{1,0:T(8,128)(2,1)S(1)} copy-done((bf16[128,1024]{1,0:T(8,128)(2,1)S(1)}, bf16[128,1024]{1,0:T(8,128)(2,1)}, u32[]{:S(2)}) %copy-start.1) | copy-done | bytes 262168
  3.8 0.0 copy-start.2
  3.8 0.9 %copy-done.2 = bf16[1,64,1024]{2,1,0:T(8,128)(2,1)S(1)} copy-done((bf16[1,64,1024]{2,1,0:T(8,128)(2,1)S(1)}, bf16[1,64,1024]{2,1,0:T(8,128)(2,1)}, u32[]{:S(2)}) %copy-start.2) | copy-done | bytes 131096
  4.7 0.0 copy-start.3
  4.7 0.9 %copy-done.3 = bf16[1,64,1024]{2,1,0:T(8,128)(2,1)S(1)} copy-done((bf16[1,64,1024]{2,1,0:T(8,128)(2,1)S(1)}, bf16[1,64,1024]{2,1,0:T(8,128)(2,1)}, u32[]{:S(2)}) %copy-start.3) | copy-done | bytes 131096
  5.6 0.0 copy-start.4
  5.6 0.8 %copy-done.4 = bf16[1,8192]{1,0:T(2,128)(2,1)S(1)} copy-done((bf16[1,8192]{1,0:T(2,128)(2,1)S(1)}, bf16[1,8192]{1,0:T(2,128)(2,1)}, u32[]{:S(2)}) %copy-start.4) | copy-done | bytes 16408
  6.4 0.0 copy-start.5
  6.4 0.7 %copy-done.5 = bf16[1,4096]{1,0:T(2,128)(2,1)S(1)} copy-done((bf16[1,4096]{1,0:T(2,128)(2,1)S(1)}, bf16[1,4096]{1,0:T(2,128)(2,1)}, u32[]{:S(2)}) %copy-start.5) | copy-done | bytes 8216
  7.1 0.0 copy-start.6
  7.1 0.7 %copy-done.6 = bf16[8192]{0:T(1024)(128)(2,1)S(1)} copy-done((bf16[8192]{0:T(1024)(128)(2,1)S(1)}, bf16[8192]{0:T(1024)(128)(2,1)}, u32[]{:S(2)}) %copy-start.6) | copy-done | bytes 16408
  7.8 0.0 copy-start.7
  7.8 0.7 %copy-done.7 = bf16[1,1024]{1,0:T(2,128)(2,1)S(1)} copy-done((bf16[1,1024]{1,0:T(2,128)(2,1)S(1)}, bf16[1,1024]{1,0:T(2,128)(2,1)}, u32[]{:S(2)}) %copy-start.7) | copy-done | bytes 2072
  8.5 0.0 copy-start.8
  8.5 0.7 %copy-done.8 = bf16[1,1024]{1,0:T(2,128)(2,1)S(1)} copy-done((bf16[1,1024]{1,0:T(2,128)(2,1)S(1)}, bf16[1,1024]{1,0:T(2,128)(2,1)}, u32[]{:S(2)}) %copy-start.8) | copy-done | bytes 2072
  9.2 19.7 %shard_map.131 = (bf16[1,8192]{1,0:T(2,128)(2,1)S(1)}, bf16[1,8192]{1,0:T(2,128)(2,1)S(1)}) custom-call(s32[1]{0:T(128)S(6)} %copy.16.plen_ref, s32[1]{0:T(128)S(6)} %copy.17.slen_ref, bf16[1,4096]{1,0:T(2,128)(2,1)S(1)} %copy-done.5, bf16[1,1024]{1,0:T(2,128)(2,1)S(1)} %copy-done.7, bf16[1,1024]{1,0:T(2,128)(2,1)S(1)} %copy-done.8, ...), custom_call_target="tpu_custom_call" | custom-call | tf_op jit(solution)/shard_map/pallas_call | solution.py:305
  28.9 0.6 %copy.18 = bf16[1,8192]{1,0:T(2,128)(2,1)} copy(bf16[1,8192]{1,0:T(2,128)(2,1)S(1)} %get-tuple-element.4) | data formatting | bytes 32768
  29.5 0.6 %copy.19 = bf16[1,8192]{1,0:T(2,128)(2,1)} copy(bf16[1,8192]{1,0:T(2,128)(2,1)S(1)} %get-tuple-element.5) | data formatting | bytes 32768
Async XLA Ops:
  1.9 1.0 %copy-start = (bf16[128,1024]{1,0:T(8,128)(2,1)S(1)}, bf16[128,1024]{1,0:T(8,128)(2,1)}, u32[]{:S(2)}) copy-start(bf16[128,1024]{1,0:T(8,128)(2,1)} %pk_hbm.1) | copy-start | bytes 786436
  2.9 0.9 %copy-start.1 = (bf16[128,1024]{1,0:T(8,128)(2,1)S(1)}, bf16[128,1024]{1,0:T(8,128)(2,1)}, u32[]{:S(2)}) copy-start(bf16[128,1024]{1,0:T(8,128)(2,1)} %pv_hbm.1) | copy-start | bytes 786436
  3.8 0.9 %copy-start.2 = (bf16[1,64,1024]{2,1,0:T(8,128)(2,1)S(1)}, bf16[1,64,1024]{2,1,0:T(8,128)(2,1)}, u32[]{:S(2)}) copy-start(bf16[1,64,1024]{2,1,0:T(8,128)(2,1)} %sk_hbm.1) | copy-start | bytes 393220
  4.7 0.9 %copy-start.3 = (bf16[1,64,1024]{2,1,0:T(8,128)(2,1)S(1)}, bf16[1,64,1024]{2,1,0:T(8,128)(2,1)}, u32[]{:S(2)}) copy-start(bf16[1,64,1024]{2,1,0:T(8,128)(2,1)} %sv_hbm.1) | copy-start | bytes 393220
  5.6 0.8 %copy-start.4 = (bf16[1,8192]{1,0:T(2,128)(2,1)S(1)}, bf16[1,8192]{1,0:T(2,128)(2,1)}, u32[]{:S(2)}) copy-start(bf16[1,8192]{1,0:T(2,128)(2,1)} %res_hbm.1) | copy-start | bytes 49156
  6.4 0.7 %copy-start.5 = (bf16[1,4096]{1,0:T(2,128)(2,1)S(1)}, bf16[1,4096]{1,0:T(2,128)(2,1)}, u32[]{:S(2)}) copy-start(bf16[1,4096]{1,0:T(2,128)(2,1)} %q_hbm.1) | copy-start | bytes 24580
  7.1 0.7 %copy-start.6 = (bf16[8192]{0:T(1024)(128)(2,1)S(1)}, bf16[8192]{0:T(1024)(128)(2,1)}, u32[]{:S(2)}) copy-start(bf16[8192]{0:T(1024)(128)(2,1)} %param.23) | copy-start | bytes 49156
  7.8 0.7 %copy-start.7 = (bf16[1,1024]{1,0:T(2,128)(2,1)S(1)}, bf16[1,1024]{1,0:T(2,128)(2,1)}, u32[]{:S(2)}) copy-start(bf16[1,1024]{1,0:T(2,128)(2,1)} %kn_hbm.1) | copy-start | bytes 6148
  8.5 0.7 %copy-start.8 = (bf16[1,1024]{1,0:T(2,128)(2,1)S(1)}, bf16[1,1024]{1,0:T(2,128)(2,1)}, u32[]{:S(2)}) copy-start(bf16[1,1024]{1,0:T(2,128)(2,1)} %vn_hbm.1) | copy-start | bytes 6148

commit v2 on v1

--- a/solution.py
+++ b/solution.py
@@ -23,8 +23,8 @@
 
 def kernel(
     n,
-    plen_ref,
-    slen_ref,
+    plen_hbm,
+    slen_hbm,
     q_hbm,
     kn_hbm,
     vn_hbm,
@@ -37,6 +37,8 @@
     gain_hbm,
     hid_ref,
     nrm_ref,
+    plen_ref,
+    slen_ref,
     qbuf,
     kn,
     vn,
@@ -93,6 +95,8 @@
                 (pv_hbm, pv),
                 (res_hbm, res),
                 (gain_hbm, gain),
+                (slen_hbm, slen_ref),
+                (plen_hbm, plen_ref),
             )
         )
     ]
@@ -143,6 +147,7 @@
         s_suf = jnp.where(head_of_row == k, scores, s_suf)
         key_rows = jnp.where(head_of_row == k, head(kn, k).astype(jnp.float32), key_rows)
     s_new = jnp.sum(own * key_rows, axis=1, keepdims=True) * scale
+    local[9].wait()
     svalid = lax.broadcasted_iota(jnp.int32, (HQ, suf), 1) < slen_ref[0]
     s_suf = jnp.where(svalid, s_suf * scale, LOW)
     top = jnp.maximum(jnp.max(s_suf, axis=1, keepdims=True), s_new)
@@ -184,6 +189,7 @@
         ],
         axis=0,
     )
+    local[10].wait()
     pvalid = me * pre + lax.broadcasted_iota(jnp.int32, (rows, pre), 1) < plen_ref[0]
     s_pre = jnp.where(pvalid, s_pre * scale, LOW)
     top0 = m0[...]
@@ -298,7 +304,6 @@
     rows = HQ * n
     bf, f32 = jnp.bfloat16, jnp.float32
     gain = norm_gain.reshape(frows, LANES)
-    smem = pl.BlockSpec(memory_space=pltpu.SMEM)
     hbm = pl.BlockSpec(memory_space=pltpu.HBM)
     vmem = pl.BlockSpec(memory_space=pltpu.VMEM)
     dma = pltpu.SemaphoreType.DMA
@@ -308,9 +313,11 @@
             jax.ShapeDtypeStruct(residual.shape, bf),
             jax.ShapeDtypeStruct(residual.shape, bf),
         ),
-        in_specs=[smem, smem] + [hbm] * 10,
+        in_specs=[hbm] * 12,
         out_specs=(vmem, vmem),
         scratch_shapes=[
+            pltpu.SMEM(prefix_len.shape, jnp.int32),
+            pltpu.SMEM(suffix_len.shape, jnp.int32),
             pltpu.VMEM((n,) + query_new.shape, bf),
             pltpu.VMEM(key_new.shape, bf),
             pltpu.VMEM(value_new.shape, bf),
@@ -330,7 +337,7 @@
             pltpu.VMEM((n * frows, LANES), f32),
             pltpu.VMEM((n, frows, LANES), bf),
             pltpu.VMEM((n, frows, LANES), bf),
-            dma((9,)),
+            dma((11,)),
             dma((CHUNKS,)),
             dma((n - 1,)),
             dma((n - 1,)),
@@ -340,7 +347,7 @@
             dma((CHUNKS * (n - 1),)),
         ],
         compiler_params=pltpu.CompilerParams(
-            collective_id=0, has_side_effects=True, vmem_limit_bytes=40 * 1024 * 1024
+            collective_id=0, has_side_effects=True, vmem_limit_bytes=62 * 1024 * 1024
         ),
     )(
         prefix_len,

time: 30.6 us -> 25.2 us (0.82)
  local copies, waits for them, and re-layouts: 8.5 us -> 2.81 us
  Pallas kernels: 19.7 us -> 20.1 us
    unnamed x20 -> x2, local copies, waits for them, and re-layouts: 8.5 us -> 2.81 us
    pallas_call x1, Pallas kernels: 19.7 us -> 20.1 us  [local(): pl.pallas_call(functools.partial(kernel, n), out_shape=(jax.ShapeDtypeStr...]
where the time goes in v2:
time: 25.2 us; the launch traced here: 24.9 us
  Pallas kernels  20.1 us (80%)
  local copies, waits for them, and re-layouts  2.81 us (11%)
  between operations  1.93 us (8%)
    pallas_call x1, Pallas kernels, local(): pl.pallas_call(functools.partial(kernel, n), out_shape=(jax.ShapeDtypeStr...  20.1 us
    unnamed x2, local copies, waits for them, and re-layouts  2.81 us

profile of v2, /device:TPU:0, one launch (start us, length us, event | category | flops | bytes accessed | tf_op | source)
XLA Modules:
  0.0 24.9 jit_solution(3591891193228604352)
XLA Ops:
  1.9 20.1 %shard_map.131 = (bf16[1,8192]{1,0:T(2,128)(2,1)}, bf16[1,8192]{1,0:T(2,128)(2,1)}) custom-call(s32[1]{0:T(128)S(6)} %copy.16.plen_hbm, s32[1]{0:T(128)S(6)} %copy.17.slen_hbm, bf16[1,4096]{1,0:T(2,128)(2,1)} %q_hbm.1, bf16[1,1024]{1,0:T(2,128)(2,1)} %kn_hbm.1, bf16[1,1024]{1,0:T(2,128)(2,1)} %vn_hbm.1, bf16[128,1024]{1,0:T(8,128)(2,1)} %pk_hbm.1, ...), custom_call_target="tpu_custom_call" | custom-call | tf_op jit(solution)/shard_map/pallas_call | solution.py:310
  22.1 1.4 %copy.18 = bf16[1,8192]{1,0:T(2,128)(2,1)} copy(bf16[1,8192]{1,0:T(2,128)(2,1)} %get-tuple-element.4) | data formatting | bytes 32768
  23.5 1.4 %copy.19 = bf16[1,8192]{1,0:T(2,128)(2,1)} copy(bf16[1,8192]{1,0:T(2,128)(2,1)} %get-tuple-element.5) | data formatting | bytes 32768

commit v3 on v2

--- a/solution.py
+++ b/solution.py
@@ -310,8 +310,8 @@
     return pl.pallas_call(
         functools.partial(kernel, n),
         out_shape=(
-            jax.ShapeDtypeStruct(residual.shape, bf),
-            jax.ShapeDtypeStruct(residual.shape, bf),
+            pltpu.VMEM(residual.shape, bf),
+            pltpu.VMEM(residual.shape, bf),
         ),
         in_specs=[hbm] * 12,
         out_specs=(vmem, vmem),

time: 25.2 us -> 22.8 us (0.905)
  local copies, waits for them, and re-layouts: 2.81 us -> 1.23 us
  Pallas kernels: 20.1 us -> 19.5 us
    unnamed x2, local copies, waits for them, and re-layouts: 2.81 us -> 1.23 us
    pallas_call x1, Pallas kernels: 20.1 us -> 19.5 us  [local(): pl.pallas_call(functools.partial(kernel, n), out_shape=(pltpu.VMEM(residu...]
where the time goes in v3:
time: 22.8 us; the launch traced here: 22.7 us
  Pallas kernels  19.5 us (86%)
  between operations  1.93 us (8%)
  local copies, waits for them, and re-layouts  1.23 us (5%)
    pallas_call x1, Pallas kernels, local(): pl.pallas_call(functools.partial(kernel, n), out_shape=(pltpu.VMEM(residu...  19.5 us
    unnamed x2, local copies, waits for them, and re-layouts  1.23 us

profile of v3, /device:TPU:0, one launch (start us, length us, event | category | flops | bytes accessed | tf_op | source)
XLA Modules:
  0.0 22.7 jit_solution(18347568968255958003)
XLA Ops:
  1.9 19.5 %shard_map.131 = (bf16[1,8192]{1,0:T(2,128)(2,1)S(1)}, bf16[1,8192]{1,0:T(2,128)(2,1)S(1)}) custom-call(s32[1]{0:T(128)S(6)} %copy.18.plen_hbm, s32[1]{0:T(128)S(6)} %copy.19.slen_hbm, bf16[1,4096]{1,0:T(2,128)(2,1)} %q_hbm.1, bf16[1,1024]{1,0:T(2,128)(2,1)} %kn_hbm.1, bf16[1,1024]{1,0:T(2,128)(2,1)} %vn_hbm.1, bf16[128,1024]{1,0:T(8,128)(2,1)} %pk_hbm.1, ...), custom_call_target="tpu_custom_call" | custom-call | tf_op jit(solution)/shard_map/pallas_call | solution.py:310
  21.4 0.6 %copy.16 = bf16[1,8192]{1,0:T(2,128)(2,1)} copy(bf16[1,8192]{1,0:T(2,128)(2,1)S(1)} %get-tuple-element.2) | data formatting | bytes 32768
  22.1 0.6 %copy.17 = bf16[1,8192]{1,0:T(2,128)(2,1)} copy(bf16[1,8192]{1,0:T(2,128)(2,1)S(1)} %get-tuple-element.3) | data formatting | bytes 32768

commit v4 on v3

--- a/solution.py
+++ b/solution.py
@@ -55,6 +55,8 @@
     o0,
     pbuf,
     rbuf,
+    tbuf,
+    trecv,
     yacc,
     ysend,
     ybuf,
@@ -62,6 +64,8 @@
     w_sem,
     q_send,
     q_recv,
+    t_send,
+    t_recv,
     p_send,
     p_recv,
     y_send,
@@ -116,25 +120,10 @@
         pl.semaphore_signal(
             barrier, inc=1, device_id={"mp": peer(d)}, device_id_type=pl.DeviceIdType.MESH
         )
-    pl.semaphore_wait(barrier, n - 1)
-
-    local[0].wait()
-    q_copies = []
-    for d in range(1, n):
-        copy = pltpu.make_async_remote_copy(
-            src_ref=qbuf.at[me],
-            dst_ref=qbuf.at[me],
-            send_sem=q_send.at[d - 1],
-            recv_sem=q_recv.at[d - 1],
-            device_id={"mp": peer(d)},
-            device_id_type=pl.DeviceIdType.MESH,
-        )
-        copy.start()
-        q_copies.append(copy)
-
     m0[...] = jnp.full(m0.shape, LOW, jnp.float32)
     l0[...] = jnp.zeros(l0.shape, jnp.float32)
     o0[...] = jnp.zeros(o0.shape, jnp.float32)
+    local[0].wait()
     own = qbuf[me].astype(jnp.float32).reshape(HQ, HEAD_SIZE)
     own_bf = own.astype(jnp.bfloat16)
     head_of_row = lax.broadcasted_iota(jnp.int32, (HQ, 1), 0) // GROUP
@@ -169,6 +158,21 @@
     l0[own_at, :] = jnp.broadcast_to(own_total, (HQ, LANES))
     o0[own_at, :] = own_sum
 
+    pl.semaphore_wait(barrier, n - 1)
+
+    q_copies = []
+    for d in range(1, n):
+        copy = pltpu.make_async_remote_copy(
+            src_ref=qbuf.at[me],
+            dst_ref=qbuf.at[me],
+            send_sem=q_send.at[d - 1],
+            recv_sem=q_recv.at[d - 1],
+            device_id={"mp": peer(d)},
+            device_id_type=pl.DeviceIdType.MESH,
+        )
+        copy.start()
+        q_copies.append(copy)
+
     local[5].wait()
     local[6].wait()
     for copy in q_copies:
@@ -199,6 +203,26 @@
     keep = jnp.exp(top0 - top)
     total = jnp.sum(w_pre, axis=1, keepdims=True) + l0[...] * keep
     w_bf = w_pre.astype(jnp.bfloat16)
+    diagonal = lax.broadcasted_iota(jnp.int32, (part_rows, LANES), 0) == lax.broadcasted_iota(
+        jnp.int32, (part_rows, LANES), 1
+    )
+    for s in range(n):
+        at = slice(s * part_rows, (s + 1) * part_rows)
+        for i, column in enumerate((top, total)):
+            tbuf[s, i : i + 1, :] = jnp.sum(
+                jnp.where(diagonal, column[at], 0.0), axis=0, keepdims=True
+            )
+    t_copies = []
+    for d in range(1, n):
+        copy = pltpu.make_async_remote_copy(
+            src_ref=tbuf.at[peer(d)],
+            dst_ref=trecv.at[me],
+            send_sem=t_send.at[d - 1],
+            recv_sem=t_recv.at[d - 1],
+            device_id={"mp": peer(d)},
+            device_id_type=pl.DeviceIdType.MESH,
+        )
+        t_copies.append(copy)
     sums = jnp.concatenate(
         [
             jnp.dot(
@@ -211,11 +235,9 @@
         axis=0,
     )
     sums = sums + o0[...] * keep
-    high = total.astype(jnp.bfloat16).astype(jnp.float32)
-    lane = lax.broadcasted_iota(jnp.int32, (rows, LANES), 1)
-    stats = jnp.where(lane < 32, top, jnp.where(lane < 64, high, total - high))
-    pbuf[:, :LANES] = sums.astype(jnp.bfloat16)
-    pbuf[:, LANES:] = stats.astype(jnp.bfloat16)
+    pbuf[...] = sums.astype(jnp.bfloat16)
+    for copy in t_copies:
+        copy.start()
 
     p_copies = []
     for d in range(1, n):
@@ -230,19 +252,22 @@
         copy.start()
         p_copies.append(copy)
     rbuf[me] = pbuf[pl.ds(pl.multiple_of(me * part_rows, part_rows), part_rows), :]
+    trecv[me] = tbuf[me]
+    for copy in t_copies:
+        copy.wait_recv()
+
+    tops = [trecv[s, 0:1, :] for s in range(n)]
+    best = functools.reduce(jnp.maximum, tops)
+    factors = [jnp.exp(top_s - best) for top_s in tops]
+    whole_total = sum(factors[s] * trecv[s, 1:2, :] for s in range(n))
+    columns = [
+        jnp.sum(jnp.where(diagonal, row, 0.0), axis=1, keepdims=True)
+        for row in factors + [whole_total]
+    ]
     for copy in p_copies:
         copy.wait_recv()
-
-    stats = [rbuf[s, :, LANES:].astype(jnp.float32) for s in range(n)]
-    tops = [st[:, 0:1] for st in stats]
-    best = functools.reduce(jnp.maximum, tops)
-    whole_total = jnp.zeros((part_rows, 1), jnp.float32)
-    whole_sum = jnp.zeros((part_rows, HEAD_SIZE), jnp.float32)
-    for s in range(n):
-        factor = jnp.exp(tops[s] - best)
-        whole_total = whole_total + factor * (stats[s][:, 32:33] + stats[s][:, 64:65])
-        whole_sum = whole_sum + factor * rbuf[s, :, :LANES].astype(jnp.float32)
-    attn = whole_sum / whole_total
+    whole_sum = sum(columns[s] * rbuf[s].astype(jnp.float32) for s in range(n))
+    attn = whole_sum / columns[n]
     attn = jnp.concatenate([attn[h * n : (h + 1) * n] for h in range(heads_dev)], axis=1)
     attn = attn.astype(jnp.bfloat16)
 
@@ -279,7 +304,7 @@
     meansq = jnp.sum(stream * stream, keepdims=True) / width
     normed = stream * lax.rsqrt(meansq + 1e-05) * gain[...].astype(jnp.float32)
     nrm_ref[...] = normed.astype(jnp.bfloat16).reshape(nrm_ref.shape)
-    for copy in q_copies + p_copies + y_copies:
+    for copy in q_copies + t_copies + p_copies + y_copies:
         copy.wait_send()
 
 
@@ -332,13 +357,17 @@
             pltpu.VMEM((rows, LANES), f32),
             pltpu.VMEM((rows, LANES), f32),
             pltpu.VMEM((rows, HEAD_SIZE), f32),
-            pltpu.VMEM((rows, HEAD_SIZE + LANES), bf),
-            pltpu.VMEM((n, rows // n, HEAD_SIZE + LANES), bf),
+            pltpu.VMEM((rows, HEAD_SIZE), bf),
+            pltpu.VMEM((n, rows // n, HEAD_SIZE), bf),
+            pltpu.VMEM((n, 2, LANES), f32),
+            pltpu.VMEM((n, 2, LANES), f32),
             pltpu.VMEM((n * frows, LANES), f32),
             pltpu.VMEM((n, frows, LANES), bf),
             pltpu.VMEM((n, frows, LANES), bf),
             dma((11,)),
             dma((CHUNKS,)),
+            dma((n - 1,)),
+            dma((n - 1,)),
             dma((n - 1,)),
             dma((n - 1,)),
             dma((n - 1,)),

time: 22.8 us -> 23 us (level)
  no operation moved by 1% of the time
where the time goes in v4:
time: 23 us; the launch traced here: 22.7 us
  Pallas kernels  19.5 us (85%)
  between operations  1.93 us (8%)
  local copies, waits for them, and re-layouts  1.23 us (5%)
    pallas_call x1, Pallas kernels, local(): pl.pallas_call(functools.partial(kernel, n), out_shape=(pltpu.VMEM(residu...  19.5 us
    unnamed x2, local copies, waits for them, and re-layouts  1.23 us

profile of v4, /device:TPU:0, one launch (start us, length us, event | category | flops | bytes accessed | tf_op | source)
XLA Modules:
  0.0 22.7 jit_solution(4631405820852013960)
XLA Ops:
  1.9 19.5 %shard_map.131 = (bf16[1,8192]{1,0:T(2,128)(2,1)S(1)}, bf16[1,8192]{1,0:T(2,128)(2,1)S(1)}) custom-call(s32[1]{0:T(128)S(6)} %copy.18.plen_hbm, s32[1]{0:T(128)S(6)} %copy.19.slen_hbm, bf16[1,4096]{1,0:T(2,128)(2,1)} %q_hbm.1, bf16[1,1024]{1,0:T(2,128)(2,1)} %kn_hbm.1, bf16[1,1024]{1,0:T(2,128)(2,1)} %vn_hbm.1, bf16[128,1024]{1,0:T(8,128)(2,1)} %pk_hbm.1, ...), custom_call_target="tpu_custom_call" | custom-call | tf_op jit(solution)/shard_map/pallas_call | solution.py:335
  21.5 0.6 %copy.16 = bf16[1,8192]{1,0:T(2,128)(2,1)} copy(bf16[1,8192]{1,0:T(2,128)(2,1)S(1)} %get-tuple-element.2) | data formatting | bytes 32768
  22.1 0.6 %copy.17 = bf16[1,8192]{1,0:T(2,128)(2,1)} copy(bf16[1,8192]{1,0:T(2,128)(2,1)S(1)} %get-tuple-element.3) | data formatting | bytes 32768

commit v5 on v4

--- a/solution.py
+++ b/solution.py
@@ -120,10 +120,25 @@
         pl.semaphore_signal(
             barrier, inc=1, device_id={"mp": peer(d)}, device_id_type=pl.DeviceIdType.MESH
         )
+    pl.semaphore_wait(barrier, n - 1)
+
+    local[0].wait()
+    q_copies = []
+    for d in range(1, n):
+        copy = pltpu.make_async_remote_copy(
+            src_ref=qbuf.at[me],
+            dst_ref=qbuf.at[me],
+            send_sem=q_send.at[d - 1],
+            recv_sem=q_recv.at[d - 1],
+            device_id={"mp": peer(d)},
+            device_id_type=pl.DeviceIdType.MESH,
+        )
+        copy.start()
+        q_copies.append(copy)
+
     m0[...] = jnp.full(m0.shape, LOW, jnp.float32)
     l0[...] = jnp.zeros(l0.shape, jnp.float32)
     o0[...] = jnp.zeros(o0.shape, jnp.float32)
-    local[0].wait()
     own = qbuf[me].astype(jnp.float32).reshape(HQ, HEAD_SIZE)
     own_bf = own.astype(jnp.bfloat16)
     head_of_row = lax.broadcasted_iota(jnp.int32, (HQ, 1), 0) // GROUP
@@ -157,21 +172,6 @@
     m0[own_at, :] = jnp.broadcast_to(top, (HQ, LANES))
     l0[own_at, :] = jnp.broadcast_to(own_total, (HQ, LANES))
     o0[own_at, :] = own_sum
-
-    pl.semaphore_wait(barrier, n - 1)
-
-    q_copies = []
-    for d in range(1, n):
-        copy = pltpu.make_async_remote_copy(
-            src_ref=qbuf.at[me],
-            dst_ref=qbuf.at[me],
-            send_sem=q_send.at[d - 1],
-            recv_sem=q_recv.at[d - 1],
-            device_id={"mp": peer(d)},
-            device_id_type=pl.DeviceIdType.MESH,
-        )
-        copy.start()
-        q_copies.append(copy)
 
     local[5].wait()
     local[6].wait()

time: 23 us -> 22.5 us (0.978)
  Pallas kernels: 19.5 us -> 19.1 us
    pallas_call x1, Pallas kernels: 19.5 us -> 19.1 us  [local(): pl.pallas_call(functools.partial(kernel, n), out_shape=(pltpu.VMEM(residu...]
where the time goes in v5:
time: 22.5 us; the launch traced here: 22.3 us
  Pallas kernels  19.1 us (85%)
  between operations  1.93 us (9%)
  local copies, waits for them, and re-layouts  1.23 us (5%)
    pallas_call x1, Pallas kernels, local(): pl.pallas_call(functools.partial(kernel, n), out_shape=(pltpu.VMEM(residu...  19.1 us
    unnamed x2, local copies, waits for them, and re-layouts  1.23 us

profile of v5, /device:TPU:0, one launch (start us, length us, event | category | flops | bytes accessed | tf_op | source)
XLA Modules:
  0.0 22.3 jit_solution(8113064886035835899)
XLA Ops:
  1.9 19.1 %shard_map.131 = (bf16[1,8192]{1,0:T(2,128)(2,1)S(1)}, bf16[1,8192]{1,0:T(2,128)(2,1)S(1)}) custom-call(s32[1]{0:T(128)S(6)} %copy.18.plen_hbm, s32[1]{0:T(128)S(6)} %copy.19.slen_hbm, bf16[1,4096]{1,0:T(2,128)(2,1)} %q_hbm.1, bf16[1,1024]{1,0:T(2,128)(2,1)} %kn_hbm.1, bf16[1,1024]{1,0:T(2,128)(2,1)} %vn_hbm.1, bf16[128,1024]{1,0:T(8,128)(2,1)} %pk_hbm.1, ...), custom_call_target="tpu_custom_call" | custom-call | tf_op jit(solution)/shard_map/pallas_call | solution.py:335
  21.1 0.6 %copy.16 = bf16[1,8192]{1,0:T(2,128)(2,1)} copy(bf16[1,8192]{1,0:T(2,128)(2,1)S(1)} %get-tuple-element.2) | data formatting | bytes 32768
  21.7 0.6 %copy.17 = bf16[1,8192]{1,0:T(2,128)(2,1)} copy(bf16[1,8192]{1,0:T(2,128)(2,1)S(1)} %get-tuple-element.3) | data formatting | bytes 32768

commit v6 on v5

--- a/solution.py
+++ b/solution.py
@@ -35,8 +35,7 @@
     res_hbm,
     w_hbm,
     gain_hbm,
-    hid_ref,
-    nrm_ref,
+    out_ref,
     plen_ref,
     slen_ref,
     qbuf,
@@ -300,10 +299,10 @@
         copy.wait_recv()
     for d in range(1, n):
         stream = stream + ybuf[peer(d)].astype(jnp.float32)
-    hid_ref[...] = stream.astype(jnp.bfloat16).reshape(hid_ref.shape)
+    out_ref[0:1,:] = stream.astype(jnp.bfloat16).reshape(1,width)
     meansq = jnp.sum(stream * stream, keepdims=True) / width
     normed = stream * lax.rsqrt(meansq + 1e-05) * gain[...].astype(jnp.float32)
-    nrm_ref[...] = normed.astype(jnp.bfloat16).reshape(nrm_ref.shape)
+    out_ref[1:2,:] = normed.astype(jnp.bfloat16).reshape(1,width)
     for copy in q_copies + t_copies + p_copies + y_copies:
         copy.wait_send()
 
@@ -332,14 +331,11 @@
     hbm = pl.BlockSpec(memory_space=pltpu.HBM)
     vmem = pl.BlockSpec(memory_space=pltpu.VMEM)
     dma = pltpu.SemaphoreType.DMA
-    return pl.pallas_call(
+    o = pl.pallas_call(
         functools.partial(kernel, n),
-        out_shape=(
-            pltpu.VMEM(residual.shape, bf),
-            pltpu.VMEM(residual.shape, bf),
-        ),
+        out_shape=pltpu.VMEM((2, width), bf),
         in_specs=[hbm] * 12,
-        out_specs=(vmem, vmem),
+        out_specs=vmem,
         scratch_shapes=[
             pltpu.SMEM(prefix_len.shape, jnp.int32),
             pltpu.SMEM(suffix_len.shape, jnp.int32),
@@ -392,6 +388,7 @@
         out_weight,
         gain,
     )
+    return (o[0:1], o[1:2])
 
 
 def solution(mesh):

time: 22.5 us -> 21.9 us (0.973)
  local copies, waits for them, and re-layouts: 1.23 us -> 0.67 us
    unnamed x2 -> x0, local copies, waits for them, and re-layouts: 1.23 us -> none
    slice x0 -> x1, local copies, waits for them, and re-layouts: none -> 0.67 us  [local(): return (o[0:1], o[1:2])]
where the time goes in v6:
time: 21.9 us; the launch traced here: 21.7 us
  Pallas kernels  19.1 us (87%)
  between operations  1.93 us (9%)
  local copies, waits for them, and re-layouts  0.67 us (3%)
    pallas_call x1, Pallas kernels, local(): pl.pallas_call(functools.partial(kernel, n), out_shape=pltpu.VMEM((2, wid...  19.1 us
    slice x1, local copies, waits for them, and re-layouts, local(): return (o[0:1], o[1:2])  0.67 us

profile of v6, /device:TPU:0, one launch (start us, length us, event | category | flops | bytes accessed | tf_op | source)
XLA Modules:
  0.0 21.7 jit_solution(16522305325688443027)
XLA Ops:
  1.9 19.1 %shard_map.131 = bf16[2,8192]{1,0:T(2,128)(2,1)S(1)} custom-call(s32[1]{0:T(128)S(6)} %copy.14.plen_hbm, s32[1]{0:T(128)S(6)} %copy.15.slen_hbm, bf16[1,4096]{1,0:T(2,128)(2,1)} %q_hbm.1, bf16[1,1024]{1,0:T(2,128)(2,1)} %kn_hbm.1, bf16[1,1024]{1,0:T(2,128)(2,1)} %vn_hbm.1, bf16[128,1024]{1,0:T(8,128)(2,1)} %pk_hbm.1, bf16[128,1024]{1,0:T(8,128)(2,1)} %pv_hbm.1, ...), custom_call_target="tpu_custom_call" | custom-call | tf_op jit(solution)/shard_map/pallas_call | solution.py:334
  21.1 0.7 %fusion = (bf16[1,8192]{1,0:T(2,128)(2,1)}, bf16[1,8192]{1,0:T(2,128)(2,1)}) fusion(bf16[2,8192]{1,0:T(2,128)(2,1)S(1)} %shard_map.131), kind=kLoop, calls=%fused_computation | loop fusion | bytes 65536 | tf_op jit(solution)/shard_map/slice | solution.py:391

commit v7 on v6

--- a/solution.py
+++ b/solution.py
@@ -85,6 +85,9 @@
     def peer(d):
         return lax.rem(me + d, n)
 
+    upper = (me * 2) // n
+    order = [(1 - upper) * (n - i) + upper * i for i in range(1, n)]
+
     local = [
         pltpu.make_async_copy(src, dst, local_sem.at[i])
         for i, (src, dst) in enumerate(
@@ -123,7 +126,7 @@
 
     local[0].wait()
     q_copies = []
-    for d in range(1, n):
+    for d in order:
         copy = pltpu.make_async_remote_copy(
             src_ref=qbuf.at[me],
             dst_ref=qbuf.at[me],
@@ -212,7 +215,7 @@
                 jnp.where(diagonal, column[at], 0.0), axis=0, keepdims=True
             )
     t_copies = []
-    for d in range(1, n):
+    for d in order:
         copy = pltpu.make_async_remote_copy(
             src_ref=tbuf.at[peer(d)],
             dst_ref=trecv.at[me],
@@ -239,7 +242,7 @@
         copy.start()
 
     p_copies = []
-    for d in range(1, n):
+    for d in order:
         copy = pltpu.make_async_remote_copy(
             src_ref=pbuf.at[pl.ds(pl.multiple_of(peer(d) * part_rows, part_rows), part_rows)],
             dst_ref=rbuf.at[me],
@@ -279,7 +282,7 @@
         at = pl.ds(c * crows, crows)
         for s in range(n):
             ysend[s, at, :] = yacc[pl.ds(s * frows + c * crows, crows), :].astype(jnp.bfloat16)
-        for d in range(1, n):
+        for d in order:
             copy = pltpu.make_async_remote_copy(
                 src_ref=ysend.at[peer(d), at],
                 dst_ref=ybuf.at[me, at],

time: 21.9 us -> 21.7 us (level)
  no operation moved by 1% of the time
where the time goes in v7:
time: 21.7 us; the launch traced here: 21.6 us
  Pallas kernels  19 us (88%)
  between operations  1.93 us (9%)
  local copies, waits for them, and re-layouts  0.67 us (3%)
    pallas_call x1, Pallas kernels, local(): pl.pallas_call(functools.partial(kernel, n), out_shape=pltpu.VMEM((2, wid...  19 us
    slice x1, local copies, waits for them, and re-layouts, local(): return (o[0:1], o[1:2])  0.67 us

profile of v7, /device:TPU:0, one launch (start us, length us, event | category | flops | bytes accessed | tf_op | source)
XLA Modules:
  0.0 21.6 jit_solution(3923029199717321710)
XLA Ops:
  1.9 19.0 %shard_map.131 = bf16[2,8192]{1,0:T(2,128)(2,1)S(1)} custom-call(s32[1]{0:T(128)S(6)} %copy.14.plen_hbm, s32[1]{0:T(128)S(6)} %copy.15.slen_hbm, bf16[1,4096]{1,0:T(2,128)(2,1)} %q_hbm.1, bf16[1,1024]{1,0:T(2,128)(2,1)} %kn_hbm.1, bf16[1,1024]{1,0:T(2,128)(2,1)} %vn_hbm.1, bf16[128,1024]{1,0:T(8,128)(2,1)} %pk_hbm.1, bf16[128,1024]{1,0:T(8,128)(2,1)} %pv_hbm.1, ...), custom_call_target="tpu_custom_call" | custom-call | tf_op jit(solution)/shard_map/pallas_call | solution.py:337
  20.9 0.7 %fusion = (bf16[1,8192]{1,0:T(2,128)(2,1)}, bf16[1,8192]{1,0:T(2,128)(2,1)}) fusion(bf16[2,8192]{1,0:T(2,128)(2,1)S(1)} %shard_map.131), kind=kLoop, calls=%fused_computation | loop fusion | bytes 65536 | tf_op jit(solution)/shard_map/slice | solution.py:394
